TPU v7x, 32 devices: a whole 2x2x4 slice. The times are simulated.
32 devices in a mesh: fsdp: 4 (over y, x), ep: 8 (over z, core).
Axes of the slice: x: 2, y: 2, z: 4, core: 2. Of those that a mesh axis runs over, the one named last changes fastest.
Arguments:
- hidden_in: bfloat16 [8192, 2048], P(('fsdp', 'ep')), may hold values from -6 to 6
- norm_gain: float32 [2048], replicated, may hold values from 0.25 to 1.75
- expert_ids: int32 [8192, 8], P(('fsdp', 'ep')), may hold values from 0 to 15, all different within a row; in each aligned block of 256 rows (0 to 255, 256 to 511, ...) at most 160 rows name the same one
- expert_probs: float32 [8192, 8], P(('fsdp', 'ep')), may hold values from 0.05 to 0.25
- gate_proj: bfloat16 [16, 2048, 768], P('ep', 'fsdp'), may hold values from -0.125 to 0.125
- up_proj: bfloat16 [16, 2048, 768], P('ep', 'fsdp'), may hold values from -0.125 to 0.125
- down_proj: bfloat16 [16, 768, 2048], P('ep', None, 'fsdp'), may hold values from -0.21875 to 0.21875
Outputs:
- moe_out: bfloat16 [8192, 2048], P(('fsdp', 'ep'))
Inputs may be any that keep to these rules, and one draw needn't show every extreme that they name: `expert_ids`: within the rows of one device (aligned blocks of 256 rows) each expert id is named by at most 160 rows, and in some blocks one expert by exactly 160; the 8 ids of a row are distinct.
All inputs are finite; a program needn't handle non-finite values.
Results may differ from a plain program's by a relative error of at most 0.0025.
Values may be sent and summed in bfloat16 or wider, within the bound.
A program may use at most 128 MiB of HBM per device.

v0:
```python
import jax
import jax.numpy as jnp
from jax import lax
from jax.sharding import PartitionSpec as P


def rms_norm(hidden_in, norm_gain):
    values = hidden_in.astype(jnp.float32)
    spread = jnp.mean(values * values, axis=-1, keepdims=True)
    return (values * lax.rsqrt(spread + 1e-06) * norm_gain).astype(jnp.bfloat16)


def per_device(hidden_in, norm_gain, expert_ids, expert_probs, gate_proj, up_proj, down_proj):
    local_experts = gate_proj.shape[0]
    normed = rms_norm(hidden_in, norm_gain)
    all_experts = local_experts * lax.axis_size("ep")
    hot = expert_ids[:, :, None] == jnp.arange(all_experts, dtype=jnp.int32)
    weights = jnp.sum(jnp.where(hot, expert_probs[:, :, None], 0.0), axis=1)
    tokens = lax.all_gather(normed, "ep", axis=0, tiled=True)
    routed = lax.all_to_all(
        weights.reshape(weights.shape[0], lax.axis_size("ep"), local_experts),
        "ep",
        split_axis=1,
        concat_axis=0,
        tiled=True,
    ).reshape(tokens.shape[0], local_experts)
    total = 0.0
    gate_all = lax.all_gather(gate_proj, "fsdp", axis=1, tiled=True)
    up_all = lax.all_gather(up_proj, "fsdp", axis=1, tiled=True)
    down_all = lax.all_gather(down_proj, "fsdp", axis=2, tiled=True)
    for e in range(local_experts):
        gate = jnp.dot(tokens, gate_all[e], preferred_element_type=jnp.float32)
        up = jnp.dot(tokens, up_all[e], preferred_element_type=jnp.float32)
        act = (jax.nn.silu(gate) * up).astype(jnp.bfloat16)
        out = jnp.dot(act, down_all[e], preferred_element_type=jnp.float32).astype(jnp.bfloat16)
        total = total + out.astype(jnp.float32) * routed[:, e, None]
    combined = lax.psum_scatter(total, "ep", scatter_dimension=0, tiled=True)
    return combined.astype(jnp.bfloat16)


def solution(mesh):
    return jax.shard_map(
        per_device,
        mesh=mesh,
        in_specs=(
            P(("fsdp", "ep"), None),
            P(),
            P(("fsdp", "ep"), None),
            P(("fsdp", "ep"), None),
            P("ep", "fsdp", None),
            P("ep", "fsdp", None),
            P("ep", None, "fsdp"),
        ),
        out_specs=P(("fsdp", "ep"), None),
        check_vma=False,
    )
```

profile of v0, /device:TPU:0, one launch (start us, length us, event | category | flops | bytes accessed | tf_op | source)
XLA Modules:
  0.0 533.1 jit_solution(4729882364466384271)
XLA Ops:
  6.5 0.0 copy-start
  6.5 0.0 copy-start.1
  6.5 0.0 all-gather.7.cloned.1.call-start
  6.5 0.7 all-gather.7.cloned.1.call-update
  7.3 0.0 all-gather.5.cloned.1.call-start
  7.3 1.5 fusion.5
  8.8 2.5 fusion.7
  11.3 0.0 all-gather.5.cloned.1.call-update
  11.4 0.0 all-gather.9.cloned.1.call-start
  11.4 0.7 all-gather.9.cloned.1.call-update
  12.1 0.0 all-gather.11.cloned.1.call-start
  12.1 0.5 all-gather.11.cloned.1.call-update
  12.7 0.0 reduce-scatter.2.cloned.1.call-start
  12.7 0.0 copy-done
  12.7 0.0 copy-done.1
  12.8 11.8 %all_to_all.15 = f32[256,8,2]{0,2,1:T(2,128)S(1)} all-to-all(f32[256,8,2]{0,2,1:T(2,128)S(1)} %reshape.18), channel_id=1, replica_groups=mesh['fsdp'=4,'ep'=8] {'ep'}, dimensions={1} | all-to-all | bytes 32768 | tf_op jit(solution)/shard_map/all_to_all | solution.py:20
  24.6 57.4 %all-gather.7.cloned.1.call-done = bf16[2,2048,768]{2,1,0:T(8,128)(2,1)} async-done(((bf16[2,512,768]{2,1,0:T(8,128)(2,1)}), bf16[2,2048,768]{2,1,0:T(8,128)(2,1)}) %all-gather.7.cloned.1.call-update) | async-done | bytes 6291472 | tf_op jit(solution)/shard_map/all_gather | solution.py:28
  82.0 83.7 %all-gather.5.cloned.1.call-done = bf16[2048,2048]{1,0:T(8,128)(2,1)} async-done(((bf16[256,2048]{1,0:T(8,128)(2,1)}), bf16[2048,2048]{1,0:T(8,128)(2,1)}) %all-gather.5.cloned.1.call-update) | async-done | bytes 8388624 | tf_op jit(solution)/shard_map/all_gather | solution.py:19
  165.6 0.0 copy-start.2
  165.6 0.0 copy-start.3
  165.6 11.8 %fusion.1 = f32[2048,768]{1,0:T(8,128)} fusion(bf16[2048,2048]{1,0:T(8,128)(2,1)} %all-gather.5.cloned.1.call-done, bf16[2,2048,768]{2,1,0:T(8,128)(2,1)} %all-gather.7.cloned.1.call-done), kind=kOutput, calls=%fused_computation.7 | convolution fusion | flops 6442450944 | bytes 17825792 | tf_op jit(solution)/shard_map/dot_general | solution.py:32
  177.4 0.0 copy-done.2
  177.4 0.0 copy-done.3
  177.4 8.5 %fusion.2 = f32[2048,768]{1,0:T(8,128)} fusion(bf16[2048,2048]{1,0:T(8,128)(2,1)S(1)} %copy-done.2, bf16[2,2048,768]{2,1,0:T(8,128)(2,1)S(1)} %copy-done.3), kind=kOutput, calls=%fused_computation.11 | convolution fusion | flops 6442450944 | bytes 17825792 | tf_op jit(solution)/shard_map/dot_general | solution.py:32
  185.9 50.1 %all-gather.9.cloned.1.call-done = bf16[2,2048,768]{2,1,0:T(8,128)(2,1)} async-done(((bf16[2,512,768]{2,1,0:T(8,128)(2,1)}), bf16[2,2048,768]{2,1,0:T(8,128)(2,1)}) %all-gather.9.cloned.1.call-update) | async-done | bytes 6291472 | tf_op jit(solution)/shard_map/all_gather | solution.py:29
  236.0 71.6 %all-gather.11.cloned.1.call-done = bf16[2,768,2048]{2,1,0:T(8,128)(2,1)} async-done(((bf16[2,768,512]{2,1,0:T(8,128)(2,1)}), bf16[2,768,2048]{2,1,0:T(8,128)(2,1)}) %all-gather.11.cloned.1.call-update) | async-done | bytes 6291472 | tf_op jit(solution)/shard_map/all_gather | solution.py:30
  307.6 22.1 %fusion = bf16[2048,2048]{1,0:T(8,128)(2,1)} fusion(f32[2048,768]{1,0:T(8,128)} %fusion.2, bf16[2048,2048]{1,0:T(8,128)(2,1)} %all-gather.5.cloned.1.call-done, bf16[2,768,2048]{2,1,0:T(8,128)(2,1)} %all-gather.11.cloned.1.call-done, bf16[2,2048,768]{2,1,0:T(8,128)(2,1)} %all-gather.9.cloned.1.call-done), kind=kOutput, calls=%fused_computation.3 | convolution fusion | flops 12894339072 | bytes 29360128 | tf_op jit(solution)/shard_map/dot_general | solution.py:35
  329.7 25.8 %multiply_add_fusion = f32[2048,2048]{1,0:T(8,128)} fusion(f32[2048]{0:T(1024)S(1)} %bitcast.35, f32[2048]{0:T(1024)S(1)} %bitcast.34, bf16[2048,2048]{1,0:T(8,128)(2,1)} %fusion, f32[2048,768]{1,0:T(8,128)} %fusion.1, bf16[2048,2048]{1,0:T(8,128)(2,1)} %all-gather.5.cloned.1.call-done, bf16[2,768,2048]{2,1,0:T(8,128)(2,1)} %all-gather.11.cloned.1.call-done, ...), kind=kOutput, calls=%fused_computation | convolution fusion | flops 12919504896 | bytes 46153728 | tf_op jit(solution)/shard_map/dot_general | solution.py:35
  355.5 0.0 reduce-scatter.2.cloned.1.call-update
  355.5 168.3 %reduce-scatter.2.cloned.1.call-done = f32[256,2048]{1,0:T(8,128)} async-done(((f32[2048,2048]{1,0:T(8,128)}), f32[256,2048]{1,0:T(8,128)}) %reduce-scatter.2.cloned.1.call-update) | async-done | bytes 2097168 | tf_op jit(solution)/shard_map/reduce_scatter | solution.py:37
  523.8 2.7 convert_element_type.35
  (4 shorter events, 0.1 us)
Async XLA Ops:
  6.5 6.2 %copy-start = (f32[256,8]{0,1:T(8,128)S(1)}, f32[256,8]{0,1:T(8,128)}, u32[]{:S(2)}) copy-start(f32[256,8]{0,1:T(8,128)} %param.10) | copy-start | bytes 24580
  6.5 6.2 %copy-start.1 = (s32[256,8]{0,1:T(8,128)S(1)}, s32[256,8]{0,1:T(8,128)}, u32[]{:S(2)}) copy-start(s32[256,8]{0,1:T(8,128)} %param.9) | copy-start | bytes 24580
  6.5 75.4 %all-gather.7.cloned.1.call-start = ((), (), s32[]{:S(2)}) async-start(), calls=%async_computation.3 | async-start | bytes 7864320 | tf_op jit(solution)/shard_map/all_gather | solution.py:28
  7.3 158.4 %all-gather.5.cloned.1.call-start = ((), (), s32[]{:S(2)}) async-start(), calls=%async_computation.2 | async-start | bytes 9437184 | tf_op jit(solution)/shard_map/all_gather | solution.py:19
  11.4 224.7 %all-gather.9.cloned.1.call-start = ((), (), s32[]{:S(2)}) async-start(), calls=%async_computation.4 | async-start | bytes 7864320 | tf_op jit(solution)/shard_map/all_gather | solution.py:29
  12.1 295.5 %all-gather.11.cloned.1.call-start = ((), (), s32[]{:S(2)}) async-start(), calls=%async_computation.5 | async-start | bytes 7864320 | tf_op jit(solution)/shard_map/all_gather | solution.py:30
  12.7 511.2 %reduce-scatter.2.cloned.1.call-start = ((), (), s32[]{:S(2)}) async-start(), calls=%async_computation.6 | async-start | bytes 18874368 | tf_op jit(solution)/shard_map/reduce_scatter | solution.py:37
  165.6 11.8 %copy-start.2 = (bf16[2048,2048]{1,0:T(8,128)(2,1)S(1)}, bf16[2048,2048]{1,0:T(8,128)(2,1)}, u32[]{:S(2)}) copy-start(bf16[2048,2048]{1,0:T(8,128)(2,1)} %all-gather.5.cloned.1.call-done) | copy-start | bytes 25165828
  165.6 11.8 %copy-start.3 = (bf16[2,2048,768]{2,1,0:T(8,128)(2,1)S(1)}, bf16[2,2048,768]{2,1,0:T(8,128)(2,1)}, u32[]{:S(2)}) copy-start(bf16[2,2048,768]{2,1,0:T(8,128)(2,1)} %all-gather.7.cloned.1.call-done) | copy-start | bytes 18874372
Sparse Core Ops, SparseCore 0:
  9.2 72.7 all-gather.6
  83.6 82.0 all-gather.4
  167.5 68.5 all-gather.8
  237.7 69.8 all-gather.10
  355.6 168.1 reduce-scatter.1
where the time goes:
time: 533 us
  waiting for transfers between devices  433 us (81%)
  matrix products  68.2 us (13%)
  between operations  13.2 us (2%)
  blocking collectives  11.8 us (2%)
  other arithmetic  6.76 us (1%)
    reduce_scatter x1, waiting for transfers between devices, per_device(): combined = lax.psum_scatter(total, 'ep', scatter_dimension=0, tiled=True)  168 us
    all_gather x1, waiting for transfers between devices, per_device(): tokens = lax.all_gather(normed, 'ep', axis=0, tiled=True)  83.7 us
    all_gather x1, waiting for transfers between devices, per_device(): down_all = lax.all_gather(down_proj, 'fsdp', axis=2, tiled=True)  71.6 us
    all_gather x1, waiting for transfers between devices, per_device(): gate_all = lax.all_gather(gate_proj, 'fsdp', axis=1, tiled=True)  57.4 us
    all_gather x1, waiting for transfers between devices, per_device(): up_all = lax.all_gather(up_proj, 'fsdp', axis=1, tiled=True)  50.1 us
    dot_general x2, matrix products, per_device(): jnp.dot(act, down_all[e], preferred_element_type=jnp.float32)  47.9 us
    dot_general x2, matrix products, per_device(): gate = jnp.dot(tokens, gate_all[e], preferred_element_type=jnp.float32)  20.3 us
    all_to_all x1, blocking collectives, per_device(): lax.all_to_all(weights.reshape(weights.shape[0], lax.axis_size('ep'), loc...  11.8 us
  transfers between devices with their start and end apart: 5, of which 5 were waited for; matrix products, arithmetic and copies ran while one was open for 5% of the time, Pallas kernels for 0%

commit v1 on v0

--- a/solution.py
+++ b/solution.py
@@ -2,6 +2,16 @@
 import jax.numpy as jnp
 from jax import lax
 from jax.sharding import PartitionSpec as P
+
+
+def pass_along(x, axis, d):
+    devices = lax.axis_size(axis)
+    held, blocks = (x, [x])
+    for _ in range(devices - 1):
+        held = lax.ppermute(held, axis, [(i, (i + 1) % devices) for i in range(devices)])
+        blocks.insert(0, held)
+    row_of_blocks = jnp.concatenate(blocks, axis=d)
+    return jnp.roll(row_of_blocks, (lax.axis_index(axis) + 1) * x.shape[d], axis=d)
 
 
 def rms_norm(hidden_in, norm_gain):
@@ -26,7 +36,7 @@
     ).reshape(tokens.shape[0], local_experts)
     total = 0.0
     gate_all = lax.all_gather(gate_proj, "fsdp", axis=1, tiled=True)
-    up_all = lax.all_gather(up_proj, "fsdp", axis=1, tiled=True)
+    up_all = pass_along(up_proj, "fsdp", 1)
     down_all = lax.all_gather(down_proj, "fsdp", axis=2, tiled=True)
     for e in range(local_experts):
         gate = jnp.dot(tokens, gate_all[e], preferred_element_type=jnp.float32)

time: 533 us -> 510 us (0.957)
  waiting for transfers between devices: 433 us -> 394 us
  local copies, waits for them, and re-layouts: 0.04 us -> 16.6 us
  blocking collectives: 11.8 us -> 0 us
  starting transfers between devices: 0.16 us -> 11.2 us
    ppermute x0 -> x3, waiting for transfers between devices: none -> 141 us  [pass_along(): lax.ppermute(held, axis, [(i, (i + 1) % devices) for i in range(devices)])]
    all_gather x1, waiting for transfers between devices: 57.4 us -> 0.01 us  [per_device(): gate_all = lax.all_gather(gate_proj, 'fsdp', axis=1, tiled=True)]
    all_gather x1, waiting for transfers between devices: 83.7 us -> 27.4 us  [per_device(): tokens = lax.all_gather(normed, 'ep', axis=0, tiled=True)]
    all_gather x1 -> x0, waiting for transfers between devices: 50.1 us -> none  [per_device(): up_all = lax.all_gather(up_proj, 'fsdp', axis=1, tiled=True)]
    all_gather x1, waiting for transfers between devices: 71.6 us -> 49.9 us  [per_device(): down_all = lax.all_gather(down_proj, 'fsdp', axis=2, tiled=True)]
    unnamed x8 -> x17, local copies, waits for them, and re-layouts: 0.01 us -> 14.7 us
    all_to_all x1 -> x0, blocking collectives: 11.8 us -> none  [per_device(): lax.all_to_all(weights.reshape(weights.shape[0], lax.axis_size('ep'), loc...]
    all_to_all x0 -> x1, waiting for transfers between devices: none -> 7.01 us  [per_device(): lax.all_to_all(weights.reshape(weights.shape[0], lax.axis_size('ep'), loc...]
  transfers between devices with their start and end apart: 5 -> 8, of which waited for: 5 -> 7; matrix products, arithmetic and copies ran while one was open for 5% -> 8% of each run, Pallas kernels for 0% -> 0%
where the time goes in v1:
time: 510 us
  waiting for transfers between devices  394 us (77%)
  matrix products  68.2 us (13%)
  local copies, waits for them, and re-layouts  16.6 us (3%)
  between operations  13.2 us (3%)
  starting transfers between devices  11.2 us (2%)
  other arithmetic  6.76 us (1%)
    reduce_scatter x1, waiting for transfers between devices, per_device(): combined = lax.psum_scatter(total, 'ep', scatter_dimension=0, tiled=True)  168 us
    ppermute x3, waiting for transfers between devices, pass_along(): lax.ppermute(held, axis, [(i, (i + 1) % devices) for i in range(devices)])  141 us
    all_gather x1, waiting for transfers between devices, per_device(): down_all = lax.all_gather(down_proj, 'fsdp', axis=2, tiled=True)  49.9 us
    dot_general x2, matrix products, per_device(): jnp.dot(act, down_all[e], preferred_element_type=jnp.float32)  47.9 us
    all_gather x1, waiting for transfers between devices, per_device(): tokens = lax.all_gather(normed, 'ep', axis=0, tiled=True)  27.4 us
    dot_general x2, matrix products, per_device(): gate = jnp.dot(tokens, gate_all[e], preferred_element_type=jnp.float32)  20.3 us
    unnamed x17, local copies, waits for them, and re-layouts  14.7 us
  transfers between devices with their start and end apart: 8, of which 7 were waited for; matrix products, arithmetic and copies ran while one was open for 8% of the time, Pallas kernels for 0%

profile of v1, /device:TPU:0, one launch (start us, length us, event | category | flops | bytes accessed | tf_op | source)
XLA Modules:
  0.0 509.8 jit_solution(5096666702530249026)
XLA Ops:
  6.5 0.7 all-gather.6.cloned.1.call-update
  7.3 0.0 all-gather.4.cloned.1.call-start
  7.3 1.5 fusion.5
  8.8 2.5 fusion.7
  11.3 0.0 all-gather.4.cloned.1.call-update
  11.4 0.0 all-gather.8.cloned.1.call-start
  11.4 3.0 collective-permute-start
  14.5 55.0 %collective-permute-done = bf16[2,512,768]{2,1,0:T(8,128)(2,1)S(1)} collective-permute-done((bf16[2,512,768]{2,1,0:T(8,128)(2,1)}, bf16[2,512,768]{2,1,0:T(8,128)(2,1)S(1)}, u32[]{:S(2)}, u32[]{:S(2)}) %collective-permute-start) | collective-permute-done | bytes 1572896 | tf_op jit(solution)/shard_map/ppermute | solution.py:11
  69.4 2.4 collective-permute-start.1
  71.8 62.6 %collective-permute-done.1 = bf16[2,512,768]{2,1,0:T(8,128)(2,1)} collective-permute-done((bf16[2,512,768]{2,1,0:T(8,128)(2,1)S(1)}, bf16[2,512,768]{2,1,0:T(8,128)(2,1)}, u32[]{:S(2)}, u32[]{:S(2)}) %collective-permute-start.1) | collective-permute-done | bytes 1572896 | tf_op jit(solution)/shard_map/ppermute | solution.py:11
  134.4 0.8 collective-permute-start.2
  135.2 0.6 reshape.18
  135.8 4.9 all-to-all-start
  140.7 0.0 reduce-scatter.2.cloned.1.call-start
  140.7 7.0 %all-to-all-done = f32[256,8,2]{0,2,1:T(2,128)S(1)} async-done(((f32[256,8,2]{0,2,1:T(2,128)}), f32[256,8,2]{0,2,1:T(2,128)S(1)}, u32[]{:S(2)}, u32[]{:S(2)}) %all-to-all-start) | async-done | bytes 16416 | tf_op jit(solution)/shard_map/all_to_all | solution.py:30
  147.8 23.0 %collective-permute-done.2 = bf16[2,512,768]{2,1,0:T(8,128)(2,1)} collective-permute-done((bf16[2,512,768]{2,1,0:T(8,128)(2,1)}, bf16[2,512,768]{2,1,0:T(8,128)(2,1)}, u32[]{:S(2)}, u32[]{:S(2)}) %collective-permute-start.2) | collective-permute-done | bytes 1572896 | tf_op jit(solution)/shard_map/ppermute | solution.py:11
  170.7 2.7 constant_dynamic-update-slice_fusion.7
  173.4 2.7 constant_dynamic-update-slice_fusion.6
  176.2 1.3 constant_dynamic-update-slice_fusion.5
  177.5 1.3 constant_dynamic-update-slice_fusion.4
  178.8 2.7 constant_dynamic-update-slice_fusion.3
  181.5 2.7 constant_dynamic-update-slice_fusion.2
  184.1 1.3 constant_dynamic-update-slice_fusion.1
  185.4 1.3 constant_dynamic-update-slice_fusion
  186.7 27.4 %all-gather.4.cloned.1.call-done = bf16[2048,2048]{1,0:T(8,128)(2,1)} async-done(((bf16[256,2048]{1,0:T(8,128)(2,1)}), bf16[2048,2048]{1,0:T(8,128)(2,1)}) %all-gather.4.cloned.1.call-update) | async-done | bytes 8388624 | tf_op jit(solution)/shard_map/all_gather | solution.py:29
  214.1 11.8 %fusion.1 = f32[2048,768]{1,0:T(8,128)} fusion(bf16[2048,2048]{1,0:T(8,128)(2,1)} %all-gather.4.cloned.1.call-done, bf16[2,2048,768]{2,1,0:T(8,128)(2,1)} %all-gather.6.cloned.1.call-done), kind=kOutput, calls=%fused_computation.7 | convolution fusion | flops 6442450944 | bytes 17825792 | tf_op jit(solution)/shard_map/dot_general | solution.py:42
  225.9 8.5 %fusion.2 = f32[2048,768]{1,0:T(8,128)} fusion(bf16[2048,2048]{1,0:T(8,128)(2,1)S(1)} %copy-done.3, bf16[2,2048,768]{2,1,0:T(8,128)(2,1)S(1)} %copy-done.4), kind=kOutput, calls=%fused_computation.11 | convolution fusion | flops 6442450944 | bytes 17825792 | tf_op jit(solution)/shard_map/dot_general | solution.py:42
  234.4 49.9 %all-gather.8.cloned.1.call-done = bf16[2,768,2048]{2,1,0:T(8,128)(2,1)} async-done(((bf16[2,768,512]{2,1,0:T(8,128)(2,1)}), bf16[2,768,2048]{2,1,0:T(8,128)(2,1)}) %all-gather.8.cloned.1.call-update) | async-done | bytes 6291472 | tf_op jit(solution)/shard_map/all_gather | solution.py:40
  284.3 22.1 %fusion = bf16[2048,2048]{1,0:T(8,128)(2,1)} fusion(f32[2048,768]{1,0:T(8,128)} %fusion.2, bf16[2048,2048]{1,0:T(8,128)(2,1)} %all-gather.4.cloned.1.call-done, bf16[2,768,2048]{2,1,0:T(8,128)(2,1)} %all-gather.8.cloned.1.call-done, bf16[2,4096,768]{2,1,0:T(8,128)(2,1)} %constant_dynamic-update-slice_fusion, s32[]{:T(128)S(6)} %select_n.18), kind=kOutput, calls=%fused_computation.3 | convolution fusion | flops 12894339072 | bytes 29360132 | tf_op jit(solution)/shard_map/dot_general | solution.py:45
  306.4 25.8 %multiply_add_fusion = f32[2048,2048]{1,0:T(8,128)} fusion(f32[2048]{0:T(1024)S(1)} %bitcast.35, f32[2048]{0:T(1024)S(1)} %bitcast.34, bf16[2048,2048]{1,0:T(8,128)(2,1)} %fusion, f32[2048,768]{1,0:T(8,128)} %fusion.1, bf16[2048,2048]{1,0:T(8,128)(2,1)} %all-gather.4.cloned.1.call-done, bf16[2,768,2048]{2,1,0:T(8,128)(2,1)} %all-gather.8.cloned.1.call-done, ...), kind=kOutput, calls=%fused_computation | convolution fusion | flops 12919504896 | bytes 46153736 | tf_op jit(solution)/shard_map/dot_general | solution.py:45
  332.2 168.3 %reduce-scatter.2.cloned.1.call-done = f32[256,2048]{1,0:T(8,128)} async-done(((f32[2048,2048]{1,0:T(8,128)}), f32[256,2048]{1,0:T(8,128)}) %reduce-scatter.2.cloned.1.call-update) | async-done | bytes 2097168 | tf_op jit(solution)/shard_map/reduce_scatter | solution.py:47
  500.5 2.7 convert_element_type.35
  (17 shorter events, 0.1 us)
Async XLA Ops:
  6.5 128.6 %copy-start.1 = (f32[256,8]{0,1:T(8,128)S(1)}, f32[256,8]{0,1:T(8,128)}, u32[]{:S(2)}) copy-start(f32[256,8]{0,1:T(8,128)} %param.10) | copy-start | bytes 24580
  6.5 128.6 %copy-start.2 = (s32[256,8]{0,1:T(8,128)S(1)}, s32[256,8]{0,1:T(8,128)}, u32[]{:S(2)}) copy-start(s32[256,8]{0,1:T(8,128)} %param.9) | copy-start | bytes 24580
  6.5 180.1 %all-gather.6.cloned.1.call-start = ((), (), s32[]{:S(2)}) async-start(), calls=%async_computation.3 | async-start | bytes 7864320 | tf_op jit(solution)/shard_map/all_gather | solution.py:38
  7.3 206.8 %all-gather.4.cloned.1.call-start = ((), (), s32[]{:S(2)}) async-start(), calls=%async_computation.2 | async-start | bytes 9437184 | tf_op jit(solution)/shard_map/all_gather | solution.py:29
  11.3 166.1 %copy-start = (bf16[2,512,768]{2,1,0:T(8,128)(2,1)S(1)}, bf16[2,512,768]{2,1,0:T(8,128)(2,1)}, u32[]{:S(2)}) copy-start(bf16[2,512,768]{2,1,0:T(8,128)(2,1)} %param.12) | copy-start | bytes 4718596
  11.4 272.9 %all-gather.8.cloned.1.call-start = ((), (), s32[]{:S(2)}) async-start(), calls=%async_computation.4 | async-start | bytes 7864320 | tf_op jit(solution)/shard_map/all_gather | solution.py:40
  11.4 58.0 %collective-permute-start = (bf16[2,512,768]{2,1,0:T(8,128)(2,1)}, bf16[2,512,768]{2,1,0:T(8,128)(2,1)S(1)}, u32[]{:S(2)}, u32[]{:S(2)}) collective-permute-start(bf16[2,512,768]{2,1,0:T(8,128)(2,1)} %param.12), channel_id=1, source_target_pairs={{0,8},{8,16},{16,24},{24,0},{1,9},{9,17},{17,25},{25,1},{2,10},{10... | collective-permute-start | bytes 4718600 | tf_op jit(solution)/shard_map/ppermute | solution.py:11
  69.4 64.9 %collective-permute-start.1 = (bf16[2,512,768]{2,1,0:T(8,128)(2,1)S(1)}, bf16[2,512,768]{2,1,0:T(8,128)(2,1)}, u32[]{:S(2)}, u32[]{:S(2)}) collective-permute-start(bf16[2,512,768]{2,1,0:T(8,128)(2,1)S(1)} %collective-permute-done), channel_id=1, source_target_pairs={{0,8},{8,16},{16,24},{24,0},{1,9},{9,17},{17,25},{25,1},{2,10},{10... | collective-permute-start | bytes 4718600 | tf_op jit(solution)/shard_map/ppermute | solution.py:11
  134.4 36.4 %collective-permute-start.2 = (bf16[2,512,768]{2,1,0:T(8,128)(2,1)}, bf16[2,512,768]{2,1,0:T(8,128)(2,1)}, u32[]{:S(2)}, u32[]{:S(2)}) collective-permute-start(bf16[2,512,768]{2,1,0:T(8,128)(2,1)} %collective-permute-done.1), channel_id=1, source_target_pairs={{0,8},{8,16},{16,24},{24,0},{1,9},{9,17},{17,25},{25,1},{2,10},{10... | collective-permute-start | bytes 4718600 | tf_op jit(solution)/shard_map/ppermute | solution.py:11
  135.8 12.0 %all-to-all-start = ((f32[256,8,2]{0,2,1:T(2,128)}), f32[256,8,2]{0,2,1:T(2,128)S(1)}, u32[]{:S(2)}, u32[]{:S(2)}) async-start(f32[256,8,2]{0,2,1:T(2,128)} %reshape.18), calls=%async_computation | async-start | bytes 32768 | tf_op jit(solution)/shard_map/all_to_all | solution.py:30
  140.7 359.8 %reduce-scatter.2.cloned.1.call-start = ((), (), s32[]{:S(2)}) async-start(), calls=%async_computation.5 | async-start | bytes 18874368 | tf_op jit(solution)/shard_map/reduce_scatter | solution.py:47
  214.1 11.8 %copy-start.3 = (bf16[2048,2048]{1,0:T(8,128)(2,1)S(1)}, bf16[2048,2048]{1,0:T(8,128)(2,1)}, u32[]{:S(2)}) copy-start(bf16[2048,2048]{1,0:T(8,128)(2,1)} %all-gather.4.cloned.1.call-done) | copy-start | bytes 25165828
  214.1 11.8 %copy-start.4 = (bf16[2,2048,768]{2,1,0:T(8,128)(2,1)S(1)}, bf16[2,2048,768]{2,1,0:T(8,128)(2,1)}, u32[]{:S(2)}) copy-start(bf16[2,2048,768]{2,1,0:T(8,128)(2,1)} %all-gather.6.cloned.1.call-done) | copy-start | bytes 18874372
Sparse Core Ops, SparseCore 0:
  9.2 120.6 all-gather.5
  131.5 82.5 all-gather.3
  215.9 68.2 all-gather.7
  332.3 168.1 reduce-scatter.1
